TPU v7x, 256 devices: a whole 4x4x8 slice. The times are simulated.
256 devices in a mesh: band: 16 (over y, z_lo, core), shard: 16 (over z_hi, x).
Axes of the slice: x: 4, y: 4, z: 8 (z_hi: 4, z_lo: 2; z = z_hi * 2 + z_lo), core: 2. Of those that a mesh axis runs over, the one named last changes fastest.
Arguments:
- activations: bfloat16 [1024, 2304], P('shard'), may hold values from -6 to 6
- encoder: bfloat16 [2304, 131072], P(None, ('band', 'shard')), may hold values from -0.125 to 0.125
- encoder_bias: float32 [131072], P(('band', 'shard')), may hold values from -1 to -0.25
- decoder: bfloat16 [131072, 2304], P(('band', 'shard')), may hold values from -0.125 to 0.125
Outputs:
- losses: float32 [16], replicated
- encoder_grad: bfloat16 [2304, 131072], P(None, ('band', 'shard'))
- decoder_grad: bfloat16 [131072, 2304], P(('band', 'shard'))
All inputs are finite; a program needn't handle non-finite values.
Results may differ from a plain program's by a relative error of at most 0.006.
Values may be sent and summed in bfloat16 or wider, within the bound.
No kernel may reach another device: no remote copies, remote signals or barrier semaphores. Data moves between devices by JAX's collectives and lax.ppermute only.
A program may use at most 128 MiB of HBM per device.

v0:
```python
import jax
import jax.numpy as jnp
from jax import lax
from jax.sharding import PartitionSpec as P


def over_pieces(value, axis):
    pieces = lax.all_gather(value, axis)
    return pieces.sum(axis=0)


def on_device(activations, encoder, encoder_bias, decoder):
    band_count = lax.axis_size("band")
    local_count = activations.shape[0]
    divisor = local_count * lax.axis_size("shard") * activations.shape[1]
    gathered = lax.all_gather(activations, "shard", axis=0, tiled=True)
    preact = jnp.dot(gathered, encoder, preferred_element_type=jnp.float32) + encoder_bias
    linear = jnp.maximum(preact, 0.0)
    active = (linear * linear).astype(jnp.bfloat16)
    act_rows = active
    band_part = lax.psum_scatter(
        jnp.dot(act_rows, decoder, preferred_element_type=jnp.float32),
        "shard",
        scatter_dimension=0,
        tiled=True,
    )
    local_rows = activations.astype(jnp.float32)
    stacked = lax.all_gather(band_part[None], "band", axis=0, tiled=True)
    prefix_recon = jnp.cumsum(stacked, axis=0)
    errors_all = local_rows[None] - prefix_recon
    losses = over_pieces(jnp.sum(errors_all * errors_all, axis=(1, 2)), "shard") / divisor
    tail_sums = jnp.flip(jnp.cumsum(jnp.flip(errors_all, 0), axis=0), 0)
    suffix = lax.dynamic_index_in_dim(tail_sums, lax.axis_index("band"), 0, keepdims=False)
    upstream = (-suffix / band_count).astype(jnp.bfloat16)
    shard_rows = lax.all_gather(upstream, "shard", axis=0, tiled=True)
    act_block = jnp.einsum("rd,ld->rl", shard_rows, decoder, preferred_element_type=jnp.float32)
    act_grads = act_block
    act_rows = active
    dec_grads = jnp.einsum("rl,rd->ld", act_rows, shard_rows, preferred_element_type=jnp.float32)
    act_grads, dec_grads = (act_grads, dec_grads)
    pre_grads = (2.0 * linear * act_grads).astype(jnp.bfloat16)
    encoder_grad = jnp.einsum(
        "rd,rl->dl", gathered, pre_grads, preferred_element_type=jnp.float32
    ).astype(jnp.bfloat16)
    return (losses, encoder_grad, dec_grads.astype(jnp.bfloat16))


def solution(mesh):
    return jax.shard_map(
        on_device,
        mesh=mesh,
        in_specs=(
            P("shard", None),
            P(None, ("band", "shard")),
            P(("band", "shard")),
            P(("band", "shard"), None),
        ),
        out_specs=(P(), P(None, ("band", "shard")), P(("band", "shard"), None)),
        check_vma=False,
    )
```

profile of v0, /device:TPU:35, one launch (start us, length us, event | category | flops | bytes accessed | tf_op | source)
XLA Modules:
  0.0 439.7 jit_solution(9953187625067713702)
XLA Ops:
  7.2 0.7 all-gather.7.cloned.1.call-update
  7.9 0.0 reduce-scatter.2.cloned.1.call-start
  8.0 87.1 %all-gather.7.cloned.1.call-done = bf16[1024,2304]{1,0:T(8,128)(2,1)} async-done(((bf16[64,2304]{1,0:T(8,128)(2,1)}), bf16[1024,2304]{1,0:T(8,128)(2,1)}) %all-gather.7.cloned.1.call-update) | async-done | bytes 4718608 | tf_op jit(solution)/shard_map/all_gather | solution.py:16
  95.1 5.2 %fusion.18 = f32[1024,512]{1,0:T(8,128)S(1)} fusion(bf16[1024,2304]{1,0:T(8,128)(2,1)} %all-gather.7.cloned.1.call-done, bf16[2304,512]{1,0:T(8,128)(2,1)} %param.5), kind=kOutput, calls=%fused_computation.20 | convolution fusion | flops 2415919104 | bytes 9175040 | tf_op jit(solution)/shard_map/dot_general | solution.py:17
  100.3 1.4 copy-done.4
  101.7 5.0 %fusion.12 = f32[1024,2304]{1,0:T(8,128)} fusion(bf16[512,2304]{1,0:T(8,128)(2,1)S(1)} %copy-done, f32[1024,512]{1,0:T(8,128)S(1)} %fusion.18, f32[512]{0:T(512)S(1)} %copy-done.2), kind=kOutput, calls=%fused_computation.13 | convolution fusion | flops 2418016256 | bytes 13895680 | tf_op jit(solution)/shard_map/dot_general | solution.py:22
  106.7 0.0 all-gather.9.cloned.1.call-start
  106.8 127.4 %reduce-scatter.2.cloned.1.call-done = f32[64,2304]{1,0:T(8,128)} async-done(((f32[1024,2304]{1,0:T(8,128)}), f32[64,2304]{1,0:T(8,128)}) %reduce-scatter.2.cloned.1.call-update) | async-done | bytes 589840 | tf_op jit(solution)/shard_map/reduce_scatter | solution.py:21
  234.2 0.0 all-gather.11.cloned.1.call-start
  234.3 61.3 %all-gather.9.cloned.1.call-done = f32[1024,2304]{1,0:T(8,128)} async-done(((f32[64,2304]{1,0:T(8,128)}), f32[1024,2304]{1,0:T(8,128)}) %all-gather.9.cloned.1.call-update) | async-done | bytes 9437200 | tf_op jit(solution)/shard_map/all_gather | solution.py:28
  295.6 7.3 %multiply_reduce_fusion = (f32[16]{0:T(128)S(1)}, f32[16,64,2304]{2,1,0:T(8,128)}) fusion(f32[16,64,2304]{2,1,0:T(8,128)} %bitcast.22, f32[64,2304]{1,0:T(8,128)S(1)} %convert_element_type.24), kind=kOutput, calls=%fused_computation | output fusion | flops 42467312 | bytes 19464256 | tf_op jit(solution)/shard_map/jit(cumsum)/reduce_window_sum | solution.py:29
  302.9 8.2 %rev.7 = f32[16,64,2304]{2,1,0:T(8,128)} reverse(f32[16,64,2304]{2,1,0:T(8,128)} %get-tuple-element.10), dimensions={0} | reverse | bytes 18874368 | tf_op jit(solution)/shard_map/jit(_flip)/rev | solution.py:32
  311.2 6.6 %fusion.17 = f32[16,64,2304]{2,1,0:T(8,128)} fusion(f32[16,64,2304]{2,1,0:T(8,128)} %rev.7), kind=kOutput, calls=%fused_computation.19 | output fusion | flops 35389440 | bytes 18874368 | tf_op jit(solution)/shard_map/jit(cumsum)/reduce_window_sum | solution.py:32
  317.8 8.2 %rev.8 = f32[16,64,2304]{2,1,0:T(8,128)} reverse(f32[16,64,2304]{2,1,0:T(8,128)} %fusion.17), dimensions={0} | reverse | bytes 18874368 | tf_op jit(solution)/shard_map/jit(_flip)/rev | solution.py:32
  326.0 1.8 multiply_convert_fusion.2
  327.9 0.6 dynamic-slice
  329.1 0.2 dynamic-update-slice
  329.4 33.6 %all-reduce = f32[256]{0:T(256)S(1)} all-reduce(f32[256]{0:T(256)S(1)} %dynamic-update-slice), channel_id=3, replica_groups=mesh['band'=16,'shard'=16] {'shard'}, use_global_device_ids=true, to_apply=%add | all-reduce | flops 256 | bytes 2048
  363.0 0.1 reshape.13
  363.1 0.5 broadcast_multiply_fusion
  363.6 47.0 %all-gather.11.cloned.1.call-done = bf16[1,1024,2304]{2,1,0:T(8,128)(2,1)} async-done(((bf16[1,64,2304]{2,1,0:T(8,128)(2,1)}), bf16[1,1024,2304]{2,1,0:T(8,128)(2,1)}) %all-gather.11.cloned.1.call-update) | async-done | bytes 4718608 | tf_op jit(solution)/shard_map/all_gather | solution.py:35
  410.6 11.2 %fusion.7 = bf16[2304,512]{0,1:T(8,128)(2,1)} fusion(bf16[1024,2304]{1,0:T(8,128)(2,1)} %all-gather.7.cloned.1.call-done, f32[1024,512]{1,0:T(8,128)} %copy-done.4, bf16[512,2304]{1,0:T(8,128)(2,1)S(1)} %copy-done, bf16[1,1024,2304]{2,1,0:T(8,128)(2,1)} %all-gather.11.cloned.1.call-done, f32[512]{0:T(512)S(1)} %copy-done.2), kind=kOutput, calls=%fused_computation.8 | convolution fusion | flops 4835639296 | bytes 16254976 | tf_op jit(solution)/shard_map/rd,rl->dl/dot_general | solution.py:42
  421.8 4.3 copy.8
  426.1 7.1 %fusion.4 = bf16[512,2304]{1,0:T(8,128)(2,1)} fusion(bf16[1,1024,2304]{2,1,0:T(8,128)(2,1)} %all-gather.11.cloned.1.call-done, f32[1024,512]{1,0:T(8,128)} %copy-done.4, f32[512]{0:T(512)S(1)} %copy-done.2), kind=kOutput, calls=%fused_computation.6 | convolution fusion | flops 2419195904 | bytes 9177088 | tf_op jit(solution)/shard_map/rl,rd->ld/dot_general | solution.py:39
  (16 shorter events, 0.2 us)
Async XLA Ops:
  7.2 94.5 %copy-start = (bf16[512,2304]{1,0:T(8,128)(2,1)S(1)}, bf16[512,2304]{1,0:T(8,128)(2,1)}, u32[]{:S(2)}) copy-start(bf16[512,2304]{1,0:T(8,128)(2,1)} %param.7) | copy-start | bytes 7077892
  7.2 87.9 %all-gather.7.cloned.1.call-start = ((), (), s32[]{:S(2)}) async-start(), calls=%async_computation.1 | async-start | bytes 5013504 | tf_op jit(solution)/shard_map/all_gather | solution.py:16
  7.9 93.7 %copy-start.2 = (f32[512]{0:T(512)S(1)}, f32[512]{0:T(512)}, u32[]{:S(2)}) copy-start(f32[512]{0:T(512)} %param.6) | copy-start | bytes 6148
  7.9 226.3 %reduce-scatter.2.cloned.1.call-start = ((), (), s32[]{:S(2)}) async-start(), calls=%async_computation.2 | async-start | bytes 10027008 | tf_op jit(solution)/shard_map/reduce_scatter | solution.py:21
  100.3 1.4 copy-start.4
  106.7 127.6 %copy-start.1 = (bf16[64,2304]{1,0:T(8,128)(2,1)S(1)}, bf16[64,2304]{1,0:T(8,128)(2,1)}, u32[]{:S(2)}) copy-start(bf16[64,2304]{1,0:T(8,128)(2,1)} %param.4) | copy-start | bytes 884740
  106.7 188.9 %all-gather.9.cloned.1.call-start = ((), (), s32[]{:S(2)}) async-start(), calls=%async_computation.3 | async-start | bytes 10027008 | tf_op jit(solution)/shard_map/all_gather | solution.py:28
  234.2 176.4 %all-gather.11.cloned.1.call-start = ((), (), s32[]{:S(2)}) async-start(), calls=%async_computation.4 | async-start | bytes 5013504 | tf_op jit(solution)/shard_map/all_gather | solution.py:35
  317.8 10.1 %copy-start.3 = (u32[256]{0:T(256)S(1)}, u32[256]{0:T(256)}, u32[]{:S(2)}) copy-start(u32[256]{0:T(256)} %constant.28) | copy-start | bytes 3076
Sparse Core Ops, SparseCore 0:
  10.4 84.6 all-gather.6
  106.8 127.2 reduce-scatter.1
  236.0 59.5 all-gather.8
  328.0 82.5 all-gather.10
where the time goes:
time: 440 us
  waiting for transfers between devices  324 us (74%)
  blocking collectives  33.6 us (8%)
  matrix products  28.5 us (6%)
  local copies, waits for them, and re-layouts  23.1 us (5%)
  other arithmetic  16.3 us (4%)
  between operations  14.5 us (3%)
    reduce_scatter x1, waiting for transfers between devices, on_device(): lax.psum_scatter(jnp.dot(act_rows, decoder, preferred_element_type=jnp.fl...  127 us
    all_gather x1, waiting for transfers between devices, on_device(): gathered = lax.all_gather(activations, 'shard', axis=0, tiled=True)  87.1 us
    all_gather x1, waiting for transfers between devices, on_device(): stacked = lax.all_gather(band_part[None], 'band', axis=0, tiled=True)  61.3 us
    all_gather x1, waiting for transfers between devices, on_device(): shard_rows = lax.all_gather(upstream, 'shard', axis=0, tiled=True)  47 us
    unnamed x1, blocking collectives  33.6 us
    rev x2, local copies, waits for them, and re-layouts, on_device(): tail_sums = jnp.flip(jnp.cumsum(jnp.flip(errors_all, 0), axis=0), 0)  16.5 us
    dot_general x1, matrix products, on_device(): jnp.einsum('rd,rl->dl', gathered, pre_grads, preferred_element_type=jnp.f...  11.2 us
  transfers between devices with their start and end apart: 4, of which 4 were waited for; matrix products, arithmetic and copies ran while one was open for 0% of the time, Pallas kernels for 0%

commit v1 on v0

--- a/solution.py
+++ b/solution.py
@@ -32,7 +32,9 @@
     tail_sums = jnp.flip(jnp.cumsum(jnp.flip(errors_all, 0), axis=0), 0)
     suffix = lax.dynamic_index_in_dim(tail_sums, lax.axis_index("band"), 0, keepdims=False)
     upstream = (-suffix / band_count).astype(jnp.bfloat16)
-    shard_rows = lax.all_gather(upstream, "shard", axis=0, tiled=True)
+    shard_rows = jnp.concatenate(
+        lax.all_to_all(jnp.stack([upstream] * lax.axis_size("shard")), "shard", 0, 0), axis=0
+    )
     act_block = jnp.einsum("rd,ld->rl", shard_rows, decoder, preferred_element_type=jnp.float32)
     act_grads = act_block
     act_rows = active

time: 440 us -> 512 us (1.16)
  the two profiles are of different devices: /device:TPU:35 before, /device:TPU:58 now
where the time goes in v1:
time: 512 us; the launch traced here: 511 us
  waiting for transfers between devices  275 us (54%)
  blocking collectives  143 us (28%)
  matrix products  28.5 us (6%)
  local copies, waits for them, and re-layouts  25.6 us (5%)
  other arithmetic  15.5 us (3%)
  between operations  14.5 us (3%)
  starting transfers between devices  9.97 us (2%)
    unnamed x1, blocking collectives  143 us
    reduce_scatter x1, waiting for transfers between devices, on_device(): lax.psum_scatter(jnp.dot(act_rows, decoder, preferred_element_type=jnp.fl...  128 us
    all_gather x1, waiting for transfers between devices, on_device(): gathered = lax.all_gather(activations, 'shard', axis=0, tiled=True)  86.8 us
    all_gather x1, waiting for transfers between devices, on_device(): stacked = lax.all_gather(band_part[None], 'band', axis=0, tiled=True)  59.7 us
    rev x2, local copies, waits for them, and re-layouts, on_device(): tail_sums = jnp.flip(jnp.cumsum(jnp.flip(errors_all, 0), axis=0), 0)  16.5 us
    dot_general x1, matrix products, on_device(): jnp.einsum('rd,rl->dl', gathered, pre_grads, preferred_element_type=jnp.f...  11.3 us
  transfers between devices with their start and end apart: 4, of which 3 were waited for; matrix products, arithmetic and copies ran while one was open for 0% of the time, Pallas kernels for 0%

profile of v1, /device:TPU:58, one launch (start us, length us, event | category | flops | bytes accessed | tf_op | source)
XLA Modules:
  0.0 511.5 jit_solution(18358435343366002475)
XLA Ops:
  7.2 0.7 all-gather.5.cloned.1.call-update
  7.9 0.0 reduce-scatter.2.cloned.1.call-start
  8.0 86.8 %all-gather.5.cloned.1.call-done = bf16[1024,2304]{1,0:T(8,128)(2,1)} async-done(((bf16[64,2304]{1,0:T(8,128)(2,1)}), bf16[1024,2304]{1,0:T(8,128)(2,1)}) %all-gather.5.cloned.1.call-update) | async-done | bytes 4718608 | tf_op jit(solution)/shard_map/all_gather | solution.py:16
  94.8 5.2 %fusion.8 = f32[1024,512]{1,0:T(8,128)S(1)} fusion(bf16[1024,2304]{1,0:T(8,128)(2,1)} %all-gather.5.cloned.1.call-done, bf16[2304,512]{1,0:T(8,128)(2,1)} %param.5), kind=kOutput, calls=%fused_computation.17 | convolution fusion | flops 2415919104 | bytes 9175040 | tf_op jit(solution)/shard_map/dot_general | solution.py:17
  99.9 1.3 copy-done.4
  101.3 5.0 fusion.2
  106.3 0.0 all-gather.7.cloned.1.call-start
  106.4 127.7 %reduce-scatter.2.cloned.1.call-done = f32[64,2304]{1,0:T(8,128)} async-done(((f32[1024,2304]{1,0:T(8,128)}), f32[64,2304]{1,0:T(8,128)}) %reduce-scatter.2.cloned.1.call-update) | async-done | bytes 589840 | tf_op jit(solution)/shard_map/reduce_scatter | solution.py:21
  234.1 59.7 %all-gather.7.cloned.1.call-done = f32[1024,2304]{1,0:T(8,128)} async-done(((f32[64,2304]{1,0:T(8,128)}), f32[1024,2304]{1,0:T(8,128)}) %all-gather.7.cloned.1.call-update) | async-done | bytes 9437200 | tf_op jit(solution)/shard_map/all_gather | solution.py:28
  293.8 7.3 %multiply_reduce_fusion = (f32[16]{0:T(128)S(1)}, f32[16,64,2304]{2,1,0:T(8,128)}) fusion(f32[16,64,2304]{2,1,0:T(8,128)} %bitcast.16, f32[64,2304]{1,0:T(8,128)S(1)} %convert_element_type.22), kind=kOutput, calls=%fused_computation | output fusion | flops 42467312 | bytes 19464256 | tf_op jit(solution)/shard_map/jit(cumsum)/reduce_window_sum | solution.py:29
  301.1 8.2 %rev.7 = f32[16,64,2304]{2,1,0:T(8,128)} reverse(f32[16,64,2304]{2,1,0:T(8,128)} %get-tuple-element.10), dimensions={0} | reverse | bytes 18874368 | tf_op jit(solution)/shard_map/jit(_flip)/rev | solution.py:32
  309.3 6.5 %fusion.7 = f32[16,64,2304]{2,1,0:T(8,128)} fusion(f32[16,64,2304]{2,1,0:T(8,128)} %rev.7), kind=kOutput, calls=%fused_computation.16 | output fusion | flops 35389440 | bytes 18874368 | tf_op jit(solution)/shard_map/jit(cumsum)/reduce_window_sum | solution.py:32
  315.9 8.2 %rev.8 = f32[16,64,2304]{2,1,0:T(8,128)} reverse(f32[16,64,2304]{2,1,0:T(8,128)} %fusion.7), dimensions={0} | reverse | bytes 18874368 | tf_op jit(solution)/shard_map/jit(_flip)/rev | solution.py:32
  324.1 1.1 fusion.1
  325.2 2.6 stack.5
  327.8 9.9 %all-to-all-start = ((bf16[16,64,2304]{2,1,0:T(8,128)(2,1)}), bf16[16,64,2304]{2,1,0:T(8,128)(2,1)}, u32[]{:S(2)}, u32[]{:S(2)}) async-start(bf16[16,64,2304]{2,1,0:T(8,128)(2,1)} %stack.5), calls=%async_computation.1 | async-start | bytes 9437184 | tf_op jit(solution)/shard_map/all_to_all | solution.py:36
  337.7 0.6 dynamic-slice
  338.9 0.2 dynamic-update-slice
  339.2 142.5 %all-reduce = f32[256]{0:T(256)S(1)} all-reduce(f32[256]{0:T(256)S(1)} %dynamic-update-slice), channel_id=3, replica_groups=mesh['band'=16,'shard'=16] {'shard'}, use_global_device_ids=true, to_apply=%add | all-reduce | flops 256 | bytes 2048
  481.7 0.1 reshape.14
  481.8 0.5 broadcast_multiply_fusion
  482.3 7.1 %convolution_convert_fusion = bf16[512,2304]{1,0:T(8,128)(2,1)} fusion(bf16[1024,2304]{1,0:T(8,128)(2,1)} %bitcast.3, f32[1024,512]{1,0:T(8,128)} %copy-done.4, f32[512]{0:T(512)S(1)} %copy-done.2), kind=kOutput, calls=%fused_computation.2 | convolution fusion | flops 2419195904 | bytes 9177088 | tf_op jit(solution)/shard_map/rl,rd->ld/dot_general | solution.py:41
  489.4 11.3 %fusion = bf16[2304,512]{0,1:T(8,128)(2,1)} fusion(bf16[1024,2304]{1,0:T(8,128)(2,1)} %all-gather.5.cloned.1.call-done, f32[1024,512]{1,0:T(8,128)} %copy-done.4, bf16[1024,2304]{1,0:T(8,128)(2,1)} %bitcast.3, bf16[512,2304]{1,0:T(8,128)(2,1)S(1)} %copy-done, f32[512]{0:T(512)S(1)} %copy-done.2), kind=kOutput, calls=%fused_computation.4 | convolution fusion | flops 4835639296 | bytes 16254976 | tf_op jit(solution)/shard_map/rd,rl->dl/dot_general | solution.py:44
  500.7 4.3 copy.8
  (16 shorter events, 0.2 us)
Async XLA Ops:
  7.2 94.1 %copy-start = (bf16[512,2304]{1,0:T(8,128)(2,1)S(1)}, bf16[512,2304]{1,0:T(8,128)(2,1)}, u32[]{:S(2)}) copy-start(bf16[512,2304]{1,0:T(8,128)(2,1)} %param.7) | copy-start | bytes 7077892
  7.2 87.6 %all-gather.5.cloned.1.call-start = ((), (), s32[]{:S(2)}) async-start(), calls=%async_computation.2 | async-start | bytes 5013504 | tf_op jit(solution)/shard_map/all_gather | solution.py:16
  7.9 93.3 %copy-start.2 = (f32[512]{0:T(512)S(1)}, f32[512]{0:T(512)}, u32[]{:S(2)}) copy-start(f32[512]{0:T(512)} %param.6) | copy-start | bytes 6148
  7.9 226.1 %reduce-scatter.2.cloned.1.call-start = ((), (), s32[]{:S(2)}) async-start(), calls=%async_computation.3 | async-start | bytes 10027008 | tf_op jit(solution)/shard_map/reduce_scatter | solution.py:21
  99.9 1.3 copy-start.4
  106.3 127.8 %copy-start.1 = (bf16[64,2304]{1,0:T(8,128)(2,1)S(1)}, bf16[64,2304]{1,0:T(8,128)(2,1)}, u32[]{:S(2)}) copy-start(bf16[64,2304]{1,0:T(8,128)(2,1)} %param.4) | copy-start | bytes 884740
  106.3 187.5 %all-gather.7.cloned.1.call-start = ((), (), s32[]{:S(2)}) async-start(), calls=%async_computation.4 | async-start | bytes 10027008 | tf_op jit(solution)/shard_map/all_gather | solution.py:28
  327.8 9.9 %copy-start.3 = (u32[256]{0:T(256)S(1)}, u32[256]{0:T(256)}, u32[]{:S(2)}) copy-start(u32[256]{0:T(256)} %constant.28) | copy-start | bytes 3076
  327.8 154.5 %all-to-all-start = ((bf16[16,64,2304]{2,1,0:T(8,128)(2,1)}), bf16[16,64,2304]{2,1,0:T(8,128)(2,1)}, u32[]{:S(2)}, u32[]{:S(2)}) async-start(bf16[16,64,2304]{2,1,0:T(8,128)(2,1)} %stack.5), calls=%async_computation.1 | async-start | bytes 9437184 | tf_op jit(solution)/shard_map/all_to_all | solution.py:36
Sparse Core Ops, SparseCore 0:
  10.4 84.3 all-gather.4
  106.4 127.5 reduce-scatter.1
  235.9 57.9 all-gather.6
